TPU v7x, 128 devices: a whole 4x4x4 slice. The times are simulated.
128 devices in a mesh: dp: 32 (over y, z, core), fsdp: 4 (over x).
Axes of the slice: x: 4, y: 4, z: 4, core: 2. Of those that a mesh axis runs over, the one named last changes fastest.
Arguments:
- tokens: bfloat16 [65536, 4096], P(('dp', 'fsdp')), may hold values from -0.75 to 0.75
- doc_ids: int32 [65536], P(('dp', 'fsdp')), may hold values from 0 to 63, never falling along the last dimension, each value on 1 to 2048 neighbouring positions
- attn_gain: float32 [4096], replicated, may hold values from 0.1 to 1.9
- mlp_gain: float32 [4096], replicated, may hold values from 0.1 to 1.9
- w_query: bfloat16 [4096, 512], P(('dp', 'fsdp')), may hold values from -1 to 1
- w_key_value: bfloat16 [4096, 256], P(('dp', 'fsdp')), may hold values from -3 to 3
- w_out: bfloat16 [512, 4096], P(None, ('dp', 'fsdp')), may hold values from -0.25 to 0.25
- w_gate: bfloat16 [4096, 1024], P(('dp', 'fsdp')), may hold values from -0.09375 to 0.09375
- w_up: bfloat16 [4096, 1024], P(('dp', 'fsdp')), may hold values from -0.09375 to 0.09375
- w_down: bfloat16 [1024, 4096], P(None, ('dp', 'fsdp')), may hold values from -0.1875 to 0.1875
Outputs:
- mixed: bfloat16 [65536, 4096], P(('dp', 'fsdp'))
Inputs may be any that keep to these rules, and one draw needn't show every extreme that they name: `doc_ids`: document numbers never fall along the pack, and every document has at most 2048 tokens.
All inputs are finite; a program needn't handle non-finite values.
Results may differ from a plain program's by a relative error of at most 0.02.
The roundings to bfloat16 on the way count: a program that leaves them out, or rounds other values in their place, can miss the bound.
Values may be sent and summed in bfloat16 or wider, within the bound.
A program may use at most 128 MiB of HBM per device.

v0:
```python
import math
import jax
import jax.numpy as jnp
from jax import lax
from jax.sharding import PartitionSpec as P

SPAN = 4
EPS = 1e-05
THETA = 500000.0
NEGATIVE = -1e30


def sent_together(arrays, axis, dim, along):
    widths = [a.shape[along] for a in arrays]
    both = jnp.concatenate(arrays, axis=along)
    out = lax.all_gather(both, axis, axis=dim, tiled=True)
    return tuple(jnp.split(out, [sum(widths[:k]) for k in range(1, len(widths))], axis=along))


def shifted(array, axis, by):
    length = lax.axis_size(axis)
    pairs = [(i, i + by) for i in range(length) if 0 <= i + by < length]
    return lax.ppermute(array, axis, pairs)


def rms_scale(values, gain):
    wide = values.astype(jnp.float32)
    power = jnp.mean(wide * wide, axis=-1, keepdims=True)
    return (wide * lax.rsqrt(power + EPS) * gain).astype(jnp.bfloat16)


def rotate(values, position):
    head = values.shape[-1]
    half = head // 2
    freqs = THETA ** (-2.0 * jnp.arange(half, dtype=jnp.float32) / head)
    angle = position.astype(jnp.float32)[:, None, None] * freqs[None, None, :]
    cosine = jnp.cos(angle)
    sine = jnp.sin(angle)
    first = values[..., :half]
    second = values[..., half:]
    return jnp.concatenate(
        [first * cosine - second * sine, second * cosine + first * sine], axis=-1
    )


def head_scores(query, keys):
    return jnp.einsum("qhd,kd->hqk", query, keys, preferred_element_type=jnp.float32) / math.sqrt(
        query.shape[-1]
    )


def weigh_values(weights, values):
    return jnp.einsum(
        "hqk,kd->qhd", weights.astype(jnp.bfloat16), values, preferred_element_type=jnp.float32
    )


def attend_live(query, halo_pairs, halo_marks, own_pairs, marks, block):
    head = query.shape[-1]
    index = jnp.arange(query.shape[0], dtype=jnp.int32)
    allowed = (marks[None, :] == marks[:, None]) & (index[None, :] <= index[:, None])
    own_scores = jnp.where(allowed[None, :, :], head_scores(query, own_pairs[:, :head]), NEGATIVE)
    count = halo_marks.shape[0] // block
    live = jnp.sum(jnp.any(halo_marks.reshape(count, block) == marks[0], axis=1).astype(jnp.int32))
    peak = jnp.max(own_scores, axis=2)
    weights = jnp.exp(own_scores - peak[:, :, None])
    totals = jnp.sum(weights, axis=2)
    mixed = weigh_values(weights, own_pairs[:, head:])

    def add_block(step, carry):
        old_peak, old_totals, old_mixed = carry
        begin = (count - 1 - step) * block
        pairs = lax.dynamic_slice_in_dim(halo_pairs, begin, block, 0)
        block_marks = lax.dynamic_slice_in_dim(halo_marks, begin, block, 0)
        same = (block_marks[None, :] == marks[:, None])[None, :, :]
        scores = jnp.where(same, head_scores(query, pairs[:, :head]), NEGATIVE)
        new_peak = jnp.maximum(old_peak, jnp.max(scores, axis=2))
        factor = jnp.exp(old_peak - new_peak)
        block_weights = jnp.exp(scores - new_peak[:, :, None])
        new_totals = old_totals * factor + jnp.sum(block_weights, axis=2)
        new_mixed = old_mixed * jnp.transpose(factor)[:, :, None] + weigh_values(
            block_weights, pairs[:, head:]
        )
        return (new_peak, new_totals, new_mixed)

    peak, totals, mixed = lax.fori_loop(0, live, add_block, (peak, totals, mixed))
    return mixed / jnp.transpose(totals)[:, :, None]


def per_device(
    tokens, doc_ids, attn_gain, mlp_gain, w_query, w_key_value, w_out, w_gate, w_up, w_down
):
    rows = tokens.shape[0]
    rank = lax.axis_index(("dp", "fsdp"))
    normed = rms_scale(tokens, attn_gain)
    query_width = w_query.shape[1]
    pair_width = w_key_value.shape[1]
    head = pair_width // 2
    heads = query_width // head
    group_query, group_pair = sent_together((w_query, w_key_value), "fsdp", 0, 1)
    pieces = sent_together((group_query, group_pair), "dp", 0, 1)
    columns = normed
    query_raw = jnp.dot(columns, pieces[0], preferred_element_type=jnp.float32)
    pair_raw = jnp.dot(columns, pieces[1], preferred_element_type=jnp.float32)
    position = rank * rows + jnp.arange(rows, dtype=jnp.int32)
    query = rotate(query_raw.reshape(rows, heads, head), position).astype(jnp.bfloat16)
    keys = rotate(pair_raw[:, None, :head], position)[:, 0, :].astype(jnp.bfloat16)
    values = pair_raw[:, head:].astype(jnp.bfloat16)
    own_pairs = jnp.concatenate([keys, values], axis=1)
    marks = doc_ids + 1
    pair_pieces = []
    mark_pieces = []
    for distance in range(SPAN, 0, -1):
        moved_pairs, moved_marks = shifted((own_pairs, marks), ("dp", "fsdp"), distance)
        pair_pieces.append(moved_pairs)
        mark_pieces.append(moved_marks)
    halo_pairs = jnp.concatenate(pair_pieces, axis=0)
    halo_marks = jnp.concatenate(mark_pieces, axis=0)
    mixed = attend_live(query, halo_pairs, halo_marks, own_pairs, marks, rows)
    attended = mixed.reshape(rows, query_width).astype(jnp.bfloat16)
    projected = jnp.dot(
        attended,
        lax.all_gather(w_out, ("dp", "fsdp"), axis=1, tiled=True),
        preferred_element_type=jnp.float32,
    )
    resid = (tokens.astype(jnp.float32) + projected).astype(jnp.bfloat16)
    resid = lax.optimization_barrier(resid)
    normed_mlp = rms_scale(resid, mlp_gain)
    group_gate, group_up = sent_together((w_gate, w_up), "fsdp", 0, 1)
    pieces = sent_together((group_gate, group_up), "dp", 0, 1)
    columns = normed_mlp
    gate = jnp.dot(columns, pieces[0], preferred_element_type=jnp.float32)
    up_value = jnp.dot(columns, pieces[1], preferred_element_type=jnp.float32)
    hidden = (jax.nn.silu(gate) * up_value).astype(jnp.bfloat16)
    down = jnp.dot(
        hidden,
        lax.all_gather(w_down, ("dp", "fsdp"), axis=1, tiled=True),
        preferred_element_type=jnp.float32,
    )
    return (resid.astype(jnp.float32) + down).astype(jnp.bfloat16)


def solution(mesh):
    in_specs = (
        P(("dp", "fsdp"), None),
        P(("dp", "fsdp")),
        P(),
        P(),
        P(("dp", "fsdp"), None),
        P(("dp", "fsdp"), None),
        P(None, ("dp", "fsdp")),
        P(("dp", "fsdp"), None),
        P(("dp", "fsdp"), None),
        P(None, ("dp", "fsdp")),
    )
    out_specs = P(("dp", "fsdp"), None)
    return jax.shard_map(
        per_device, mesh=mesh, in_specs=in_specs, out_specs=out_specs, check_vma=False
    )
```

profile of v0, /device:TPU:1, one launch (start us, length us, event | category | flops | bytes accessed | tf_op | source)
XLA Modules:
  0.0 306.7 jit_solution(3767838602492783908)
XLA Ops:
  6.5 0.8 pad_maximum_fusion.6
  7.3 11.6 %all_gather.18 = bf16[128,768]{1,0:T(8,128)(2,1)} all-gather(bf16[32,768]{1,0:T(8,128)(2,1)S(1)} %pad_maximum_fusion.6), channel_id=1, replica_groups=mesh['dp'=32,'fsdp'=4] {'fsdp'}, dimensions={0}, use_global_device_ids=true | all-gather | bytes 245760 | tf_op jit(solution)/shard_map/all_gather | solution.py:16
  19.0 0.7 all-gather.7.cloned.1.call-update
  19.7 0.9 pad_maximum_fusion.4
  20.6 10.6 %all_gather.21 = bf16[128,2048]{1,0:T(8,128)(2,1)} all-gather(bf16[32,2048]{1,0:T(8,128)(2,1)S(1)} %pad_maximum_fusion.4), channel_id=1, replica_groups=mesh['dp'=32,'fsdp'=4] {'fsdp'}, dimensions={0}, use_global_device_ids=true | all-gather | bytes 655360 | tf_op jit(solution)/shard_map/all_gather | solution.py:16
  31.3 0.7 broadcast_add_fusion
  32.0 9.7 %collective-permute-start = (s32[512]{0:T(512)S(1)}, s32[512]{0:T(512)S(1)}, u32[]{:S(2)}, u32[]{:S(2)}) collective-permute-start(s32[512]{0:T(512)S(1)} %broadcast_add_fusion), channel_id=1, source_target_pairs={{0,4},{1,5},{2,6},{3,7},{4,8},{5,9},{6,10},{7,11},{8,12},{9,13},{1... | collective-permute-start | bytes 6152 | tf_op jit(solution)/shard_map/ppermute | solution.py:23
  41.7 3.9 %collective-permute-start.1 = (s32[512]{0:T(512)S(1)}, s32[512]{0:T(512)S(1)}, u32[]{:S(2)}, u32[]{:S(2)}) collective-permute-start(s32[512]{0:T(512)S(1)} %broadcast_add_fusion), channel_id=1, source_target_pairs={{0,3},{1,4},{2,5},{3,6},{4,7},{5,8},{6,9},{7,10},{8,11},{9,12},{10... | collective-permute-start | bytes 6152 | tf_op jit(solution)/shard_map/ppermute | solution.py:23
  45.6 2.2 collective-permute-start.2
  47.8 2.2 collective-permute-start.3
  50.3 3.1 %fusion.17 = f32[512]{0:T(512)S(1)} fusion(bf16[512,4096]{1,0:T(8,128)(2,1)} %param.12), kind=kLoop, calls=%fused_computation.25 | loop fusion | flops 6290944 | bytes 4196352 | tf_op jit(solution)/shard_map/reduce_sum | solution.py:28
  53.4 1.0 multiply_cosine_fusion
  54.4 0.5 slice.36
  55.0 0.7 broadcast_compare_fusion.1
  55.8 0.7 convert_reduce_fusion
  56.5 16.5 %all-gather.5.cloned.1.call-done = bf16[4096,768]{1,0:T(8,128)(2,1)} async-done(((bf16[128,768]{1,0:T(8,128)(2,1)}), bf16[4096,768]{1,0:T(8,128)(2,1)}) %all-gather.5.cloned.1.call-update) | async-done | bytes 6291472 | tf_op jit(solution)/shard_map/all_gather | solution.py:16
  73.0 4.6 %fusion.34 = f32[512,256]{0,1:T(8,128)S(1)} fusion(bf16[4096,768]{1,0:T(8,128)(2,1)} %all-gather.5.cloned.1.call-done, bf16[512,4096]{1,0:T(8,128)(2,1)} %param.12, f32[4096]{0:T(1024)S(1)} %copy-done.8, f32[512]{0:T(512)S(1)} %add_rsqrt_fusion.1), kind=kOutput, calls=%fused_computation.44 | convolution fusion | flops 1082130432 | bytes 6834176 | tf_op jit(solution)/shard_map/dot_general | solution.py:104
  77.7 0.6 fusion.54
  78.2 0.7 pad_maximum_fusion.2
  79.0 2.3 collective-permute-start.4
  81.3 4.3 %collective-permute-start.5 = (bf16[512,256]{0,1:T(8,128)(2,1)}, bf16[512,256]{0,1:T(8,128)(2,1)}, u32[]{:S(2)}, u32[]{:S(2)}) collective-permute-start(bf16[512,256]{0,1:T(8,128)(2,1)} %pad_maximum_fusion.2), channel_id=1, source_target_pairs={{0,3},{1,4},{2,5},{3,6},{4,7},{5,8},{6,9},{7,10},{8,11},{9,12},{10... | collective-permute-start | bytes 786440 | tf_op jit(solution)/shard_map/ppermute | solution.py:23
  85.6 2.4 collective-permute-start.6
  88.0 2.6 collective-permute-start.7
  90.7 2.6 fusion.29
  93.4 0.3 copy.32
  93.7 0.3 copy.33
  94.1 0.3 subtract_convert_fusion
  94.4 0.3 pad_maximum_fusion.1
  94.7 0.9 fusion.33
  95.6 1.3 fusion.41
  97.0 0.9 fusion.32
  98.0 5.3 %collective-permute-done.7 = bf16[512,256]{0,1:T(8,128)(2,1)} collective-permute-done((bf16[512,256]{0,1:T(8,128)(2,1)}, bf16[512,256]{0,1:T(8,128)(2,1)}, u32[]{:S(2)}, u32[]{:S(2)}) %collective-permute-start.7) | collective-permute-done | bytes 262176 | tf_op jit(solution)/shard_map/ppermute | solution.py:23
  103.4 1.3 pad_maximum_fusion
  104.7 9.5 %while.14 = (s32[]{:T(128)}, f32[4,512]{1,0:T(4,128)S(1)}, f32[4,512]{1,0:T(4,128)S(1)}, f32[512,4,128]{0,2,1:T(8,128)S(1)}, s32[]{:T(128)}, /*index=5*/s32[2048...) while((s32[]{:T(128)}, f32[4,512]{1,0:T(4,128)S(1)}, ...), condition=%wide.region_8.9_spmd, body=%wide.region_5.8_spmd.sunk | while | flops 549197824 | bytes 33431808 | solution.py:86
  105.4 0.2 broadcast_compare_fusion.3
  105.6 2.9 fusion.80
  108.5 3.8 %fusion.83 = f32[512,4,128]{0,2,1:T(8,128)S(1)} fusion(f32[512,512,4]{1,0,2:T(8,128)} %get-tuple-element.168, f32[4,512]{1,0:T(4,128)S(1)} %get-tuple-element.201, pred[512,512]{0,1:T(8,128)(4,1)S(1)} %broadcast_compare_fusion.3, f32[512,4,128]{0,2,1:T(8,128)S(1)} %get-tuple-element.188, f32[512,4]{0,1:T(4,128)S(1)} %get-tuple-element.169, ...), kind=kOutput, calls=%fused_computation.8.clone.1 | convolution fusion | flops 273154048 | bytes 6701064 | tf_op jit(solution)/shard_map/while/body/hqk,kd->qhd/dot_general | solution.py:53
  112.4 0.9 fusion.82
  114.3 30.9 %all-gather.7.cloned.1.call-done = bf16[512,4096]{0,1:T(8,128)(2,1)} async-done(((bf16[512,32]{0,1:T(8,128)(2,1)}), bf16[512,4096]{0,1:T(8,128)(2,1)}) %all-gather.7.cloned.1.call-update) | async-done | bytes 4194320 | tf_op jit(solution)/shard_map/all_gather | solution.py:123
  145.2 5.9 %fusion.20 = bf16[512,4096]{1,0:T(8,128)(2,1)S(1)} fusion(bf16[512,4096]{1,0:T(8,128)(2,1)} %param.12, bf16[512,512]{0,1:T(8,128)(2,1)S(1)} %bitcast.82, bf16[512,4096]{0,1:T(8,128)(2,1)} %all-gather.7.cloned.1.call-done), kind=kOutput, calls=%fused_computation.28 | convolution fusion | flops 2153775104 | bytes 13107200 | tf_op jit(solution)/shard_map/dot_general | solution.py:121
  151.1 2.0 copy-done.2
  153.1 0.9 fusion.21
  154.0 63.8 %all-gather.9.cloned.1.call-done = bf16[4096,2048]{1,0:T(8,128)(2,1)} async-done(((bf16[128,2048]{1,0:T(8,128)(2,1)}), bf16[4096,2048]{1,0:T(8,128)(2,1)}) %all-gather.9.cloned.1.call-update) | async-done | bytes 16777232 | tf_op jit(solution)/shard_map/all_gather | solution.py:16
  217.8 8.4 %fusion.27 = f32[512,1024]{1,0:T(8,128)S(1)} fusion(bf16[4096,2048]{1,0:T(8,128)(2,1)} %all-gather.9.cloned.1.call-done, bf16[512,4096]{1,0:T(8,128)(2,1)} %copy-done.2, f32[4096]{0:T(1024)S(1)} %copy-done.9, f32[512]{0:T(512)S(1)} %add_rsqrt_fusion), kind=kOutput, calls=%fused_computation.35 | convolution fusion | flops 4303355904 | bytes 14698496 | tf_op jit(solution)/shard_map/dot_general | solution.py:132
  226.3 2.3 copy-done.6
  228.6 4.7 %multiply_convert_fusion = bf16[512,1024]{1,0:T(8,128)(2,1)S(1)} fusion(f32[512,1024]{1,0:T(8,128)S(1)} %fusion.27, bf16[4096,2048]{1,0:T(8,128)(2,1)S(1)} %copy-done.6, bf16[512,4096]{1,0:T(8,128)(2,1)S(1)} %copy-done.3, f32[4096]{0:T(1024)S(1)} %copy-done.9, f32[512]{0:T(512)S(1)} %add_rsqrt_fusion), kind=kOutput, calls=%fused_computation.46 | convolution fusion | flops 4306501632 | bytes 15747072 | tf_op jit(solution)/shard_map/dot_general | solution.py:133
  233.3 56.6 %all-gather.11.cloned.1.call-done = bf16[1024,4096]{0,1:T(8,128)(2,1)} async-done(((bf16[1024,32]{0,1:T(8,128)(2,1)}), bf16[1024,4096]{0,1:T(8,128)(2,1)}) %all-gather.11.cloned.1.call-update) | async-done | bytes 8388624 | tf_op jit(solution)/shard_map/all_gather | solution.py:137
  289.9 10.2 %fusion.24 = bf16[512,4096]{1,0:T(8,128)(2,1)} fusion(bf16[512,4096]{1,0:T(8,128)(2,1)} %copy-done.2, bf16[512,1024]{1,0:T(8,128)(2,1)S(1)} %multiply_convert_fusion, bf16[1024,4096]{0,1:T(8,128)(2,1)} %all-gather.11.cloned.1.call-done), kind=kOutput, calls=%fused_computation.32 | convolution fusion | flops 4301258752 | bytes 17825792 | tf_op jit(solution)/shard_map/dot_general | solution.py:135
  (53 shorter events, 1.2 us)
Async XLA Ops:
  6.5 66.5 %copy-start.8 = (f32[4096]{0:T(1024)S(1)}, f32[4096]{0:T(1024)}, u32[]{:S(2)}) copy-start(f32[4096]{0:T(1024)} %param.14) | copy-start | bytes 49156
  6.5 66.5 %all-gather.5.cloned.1.call-start = ((), (), s32[]{:S(2)}) async-start(), calls=%async_computation | async-start | bytes 6488064 | tf_op jit(solution)/shard_map/all_gather | solution.py:16
  18.9 126.3 %all-gather.7.cloned.1.call-start = ((), (), s32[]{:S(2)}) async-start(), calls=%async_computation.1 | async-start | bytes 4227072 | tf_op jit(solution)/shard_map/all_gather | solution.py:123
  19.7 198.2 %all-gather.9.cloned.1.call-start = ((), (), s32[]{:S(2)}) async-start(), calls=%async_computation.2 | async-start | bytes 17301504 | tf_op jit(solution)/shard_map/all_gather | solution.py:16
  31.3 258.7 %all-gather.11.cloned.1.call-start = ((), (), s32[]{:S(2)}) async-start(), calls=%async_computation.3 | async-start | bytes 8454144 | tf_op jit(solution)/shard_map/all_gather | solution.py:137
  32.0 22.9 %collective-permute-start = (s32[512]{0:T(512)S(1)}, s32[512]{0:T(512)S(1)}, u32[]{:S(2)}, u32[]{:S(2)}) collective-permute-start(s32[512]{0:T(512)S(1)} %broadcast_add_fusion), channel_id=1, source_target_pairs={{0,4},{1,5},{2,6},{3,7},{4,8},{5,9},{6,10},{7,11},{8,12},{9,13},{1... | collective-permute-start | bytes 6152 | tf_op jit(solution)/shard_map/ppermute | solution.py:23
  41.7 13.2 %collective-permute-start.1 = (s32[512]{0:T(512)S(1)}, s32[512]{0:T(512)S(1)}, u32[]{:S(2)}, u32[]{:S(2)}) collective-permute-start(s32[512]{0:T(512)S(1)} %broadcast_add_fusion), channel_id=1, source_target_pairs={{0,3},{1,4},{2,5},{3,6},{4,7},{5,8},{6,9},{7,10},{8,11},{9,12},{10... | collective-permute-start | bytes 6152 | tf_op jit(solution)/shard_map/ppermute | solution.py:23
  45.6 9.3 %collective-permute-start.2 = (s32[512]{0:T(512)S(1)}, s32[512]{0:T(512)S(1)}, u32[]{:S(2)}, u32[]{:S(2)}) collective-permute-start(s32[512]{0:T(512)S(1)} %broadcast_add_fusion), channel_id=1, source_target_pairs={{0,2},{1,3},{2,4},{3,5},{4,6},{5,7},{6,8},{7,9},{8,10},{9,11},{10,... | collective-permute-start | bytes 6152 | tf_op jit(solution)/shard_map/ppermute | solution.py:23
  47.8 7.1 %collective-permute-start.3 = (s32[512]{0:T(512)S(1)}, s32[512]{0:T(512)S(1)}, u32[]{:S(2)}, u32[]{:S(2)}) collective-permute-start(s32[512]{0:T(512)S(1)} %broadcast_add_fusion), channel_id=1, source_target_pairs={{0,1},{1,2},{2,3},{3,4},{4,5},{5,6},{6,7},{7,8},{8,9},{9,10},{10,1... | collective-permute-start | bytes 6152 | tf_op jit(solution)/shard_map/ppermute | solution.py:23
  73.0 17.6 %copy-start.1 = (bf16[512,4096]{1,0:T(8,128)(2,1)S(1)}, bf16[512,4096]{1,0:T(8,128)(2,1)}, u32[]{:S(2)}) copy-start(bf16[512,4096]{1,0:T(8,128)(2,1)} %param.12) | copy-start | bytes 12582916
  73.0 17.7 %copy-start.7 = (bf16[4096,768]{1,0:T(8,128)(2,1)S(1)}, bf16[4096,768]{1,0:T(8,128)(2,1)}, u32[]{:S(2)}) copy-start(bf16[4096,768]{1,0:T(8,128)(2,1)} %all-gather.5.cloned.1.call-done) | copy-start | bytes 18874372
  77.6 10.4 %copy-start.4 = (f32[512,256]{0,1:T(8,128)}, f32[512,256]{0,1:T(8,128)S(1)}, u32[]{:S(2)}) copy-start(f32[512,256]{0,1:T(8,128)S(1)} %fusion.34) | copy-start | bytes 1572868
  79.0 18.9 %collective-permute-start.4 = (bf16[512,256]{0,1:T(8,128)(2,1)}, bf16[512,256]{0,1:T(8,128)(2,1)}, u32[]{:S(2)}, u32[]{:S(2)}) collective-permute-start(bf16[512,256]{0,1:T(8,128)(2,1)} %pad_maximum_fusion.2), channel_id=1, source_target_pairs={{0,4},{1,5},{2,6},{3,7},{4,8},{5,9},{6,10},{7,11},{8,12},{9,13},{1... | collective-permute-start | bytes 786440 | tf_op jit(solution)/shard_map/ppermute | solution.py:23
  81.3 16.6 %collective-permute-start.5 = (bf16[512,256]{0,1:T(8,128)(2,1)}, bf16[512,256]{0,1:T(8,128)(2,1)}, u32[]{:S(2)}, u32[]{:S(2)}) collective-permute-start(bf16[512,256]{0,1:T(8,128)(2,1)} %pad_maximum_fusion.2), channel_id=1, source_target_pairs={{0,3},{1,4},{2,5},{3,6},{4,7},{5,8},{6,9},{7,10},{8,11},{9,12},{10... | collective-permute-start | bytes 786440 | tf_op jit(solution)/shard_map/ppermute | solution.py:23
  85.6 12.5 %collective-permute-start.6 = (bf16[512,256]{0,1:T(8,128)(2,1)}, bf16[512,256]{0,1:T(8,128)(2,1)}, u32[]{:S(2)}, u32[]{:S(2)}) collective-permute-start(bf16[512,256]{0,1:T(8,128)(2,1)} %pad_maximum_fusion.2), channel_id=1, source_target_pairs={{0,2},{1,3},{2,4},{3,5},{4,6},{5,7},{6,8},{7,9},{8,10},{9,11},{10,... | collective-permute-start | bytes 786440 | tf_op jit(solution)/shard_map/ppermute | solution.py:23
  88.0 15.4 %collective-permute-start.7 = (bf16[512,256]{0,1:T(8,128)(2,1)}, bf16[512,256]{0,1:T(8,128)(2,1)}, u32[]{:S(2)}, u32[]{:S(2)}) collective-permute-start(bf16[512,256]{0,1:T(8,128)(2,1)} %pad_maximum_fusion.2), channel_id=1, source_target_pairs={{0,1},{1,2},{2,3},{3,4},{4,5},{5,6},{6,7},{7,8},{8,9},{9,10},{10,1... | collective-permute-start | bytes 786440 | tf_op jit(solution)/shard_map/ppermute | solution.py:23
  94.3 1.3 copy-start.5
  108.5 3.8 %copy-start = (f32[512,512,4]{1,0,2:T(8,128)S(1)}, f32[512,512,4]{1,0,2:T(8,128)}, u32[]{:S(2)}) copy-start(f32[512,512,4]{1,0,2:T(8,128)} %get-tuple-element.168) | copy-start | bytes 12582916 | tf_op jit(solution)/shard_map/while
  151.1 2.0 copy-start.2
  153.1 64.7 %copy-start.9 = (f32[4096]{0:T(1024)S(1)}, f32[4096]{0:T(1024)}, u32[]{:S(2)}) copy-start(f32[4096]{0:T(1024)} %param.15) | copy-start | bytes 49156
  217.8 8.4 %copy-start.3 = (bf16[512,4096]{1,0:T(8,128)(2,1)S(1)}, bf16[512,4096]{1,0:T(8,128)(2,1)}, u32[]{:S(2)}) copy-start(bf16[512,4096]{1,0:T(8,128)(2,1)} %copy-done.2) | copy-start | bytes 12582916
  217.8 10.7 %copy-start.6 = (bf16[4096,2048]{1,0:T(8,128)(2,1)S(1)}, bf16[4096,2048]{1,0:T(8,128)(2,1)}, u32[]{:S(2)}) copy-start(bf16[4096,2048]{1,0:T(8,128)(2,1)} %all-gather.9.cloned.1.call-done) | copy-start | bytes 50331652
Sparse Core Ops, SparseCore 0:
  19.0 53.9 all-gather.4
  76.2 69.0 all-gather.6
  147.5 70.2 all-gather.8
  220.8 69.0 all-gather.10
where the time goes:
time: 307 us
  waiting for transfers between devices  174 us (57%)
  matrix products  45.4 us (15%)
  starting transfers between devices  29.8 us (10%)
  blocking collectives  22.2 us (7%)
  other arithmetic  14.4 us (5%)
  between operations  13.5 us (4%)
  local copies, waits for them, and re-layouts  5.78 us (2%)
    all_gather x2, waiting for transfers between devices, sent_together(): out = lax.all_gather(both, axis, axis=dim, tiled=True)  80.3 us
    all_gather x1, waiting for transfers between devices, per_device(): lax.all_gather(w_down, ('dp', 'fsdp'), axis=1, tiled=True)  56.6 us
    all_gather x1, waiting for transfers between devices, per_device(): lax.all_gather(w_out, ('dp', 'fsdp'), axis=1, tiled=True)  30.9 us
    ppermute x8, starting transfers between devices, shifted(): return lax.ppermute(array, axis, pairs)  29.7 us
    all_gather x2, blocking collectives, sent_together(): out = lax.all_gather(both, axis, axis=dim, tiled=True)  22.2 us
    dot_general x1, matrix products, per_device(): jnp.dot(hidden, lax.all_gather(w_down, ('dp', 'fsdp'), axis=1, tiled=True...  10.2 us
    dot_general x1, matrix products, per_device(): gate = jnp.dot(columns, pieces[0], preferred_element_type=jnp.float32)  8.4 us
  transfers between devices with their start and end apart: 12, of which 6 were waited for; matrix products, arithmetic and copies ran while one was open for 16% of the time, Pallas kernels for 0%

commit v1 on v0

--- a/solution.py
+++ b/solution.py
@@ -120,7 +120,12 @@
     attended = mixed.reshape(rows, query_width).astype(jnp.bfloat16)
     projected = jnp.dot(
         attended,
-        lax.all_gather(w_out, ("dp", "fsdp"), axis=1, tiled=True),
+        jnp.concatenate(
+            lax.all_to_all(
+                jnp.stack([w_out] * lax.axis_size(("dp", "fsdp"))), ("dp", "fsdp"), 0, 0
+            ),
+            axis=1,
+        ),
         preferred_element_type=jnp.float32,
     )
     resid = (tokens.astype(jnp.float32) + projected).astype(jnp.bfloat16)

time: 307 us -> 283 us (0.922)
  waiting for transfers between devices: 174 us -> 137 us
  starting transfers between devices: 29.8 us -> 39.3 us
  local copies, waits for them, and re-layouts: 5.78 us -> 9.06 us
    all_gather x1 -> x0, waiting for transfers between devices: 30.9 us -> none  [per_device(): lax.all_gather(w_out, ('dp', 'fsdp'), axis=1, tiled=True)]
    all_to_all x0 -> x1, starting transfers between devices: none -> 10.4 us  [per_device(): lax.all_to_all(jnp.stack([w_out] * lax.axis_size(('dp', 'fsdp'))), ('dp',...]
    all_gather x2, waiting for transfers between devices: 80.3 us -> 74.3 us  [sent_together(): out = lax.all_gather(both, axis, axis=dim, tiled=True)]
    another operation x0 -> x1, local copies, waits for them, and re-layouts: none -> 3.3 us  [per_device(): jnp.stack([w_out] * lax.axis_size(('dp', 'fsdp')))]
  transfers between devices with their start and end apart: 12 -> 12, of which waited for: 6 -> 5; matrix products, arithmetic and copies ran while one was open for 16% -> 19% of each run, Pallas kernels for 0% -> 0%
where the time goes in v1:
time: 283 us; the launch traced here: 282 us
  waiting for transfers between devices  137 us (48%)
  matrix products  45.4 us (16%)
  starting transfers between devices  39.3 us (14%)
  blocking collectives  22.2 us (8%)
  other arithmetic  14.4 us (5%)
  between operations  13.5 us (5%)
  local copies, waits for them, and re-layouts  9.06 us (3%)
    all_gather x2, waiting for transfers between devices, sent_together(): out = lax.all_gather(both, axis, axis=dim, tiled=True)  74.3 us
    all_gather x1, waiting for transfers between devices, per_device(): lax.all_gather(w_down, ('dp', 'fsdp'), axis=1, tiled=True)  56.8 us
    ppermute x8, starting transfers between devices, shifted(): return lax.ppermute(array, axis, pairs)  28.8 us
    all_gather x2, blocking collectives, sent_together(): out = lax.all_gather(both, axis, axis=dim, tiled=True)  22.2 us
    all_to_all x1, starting transfers between devices, per_device(): lax.all_to_all(jnp.stack([w_out] * lax.axis_size(('dp', 'fsdp'))), ('dp',...  10.4 us
    dot_general x1, matrix products, per_device(): jnp.dot(hidden, lax.all_gather(w_down, ('dp', 'fsdp'), axis=1, tiled=True...  10.2 us
    dot_general x1, matrix products, per_device(): gate = jnp.dot(columns, pieces[0], preferred_element_type=jnp.float32)  8.41 us
    dot_general x1, matrix products, per_device(): jnp.dot(attended, jnp.concatenate(lax.all_to_all(jnp.stack([w_out] * lax....  5.87 us
  transfers between devices with their start and end apart: 12, of which 5 were waited for; matrix products, arithmetic and copies ran while one was open for 19% of the time, Pallas kernels for 0%

profile of v1, /device:TPU:1, one launch (start us, length us, event | category | flops | bytes accessed | tf_op | source)
XLA Modules:
  0.0 282.2 jit_solution(9416689780375060481)
XLA Ops:
  6.5 0.8 pad_maximum_fusion.6
  7.3 11.6 %all_gather.15 = bf16[128,768]{1,0:T(8,128)(2,1)} all-gather(bf16[32,768]{1,0:T(8,128)(2,1)S(1)} %pad_maximum_fusion.6), channel_id=1, replica_groups=mesh['dp'=32,'fsdp'=4] {'fsdp'}, dimensions={0}, use_global_device_ids=true | all-gather | bytes 245760 | tf_op jit(solution)/shard_map/all_gather | solution.py:16
  19.0 0.9 pad_maximum_fusion.4
  19.8 10.6 %all_gather.17 = bf16[128,2048]{1,0:T(8,128)(2,1)} all-gather(bf16[32,2048]{1,0:T(8,128)(2,1)S(1)} %pad_maximum_fusion.4), channel_id=1, replica_groups=mesh['dp'=32,'fsdp'=4] {'fsdp'}, dimensions={0}, use_global_device_ids=true | all-gather | bytes 655360 | tf_op jit(solution)/shard_map/all_gather | solution.py:16
  30.5 0.7 broadcast_add_fusion
  31.2 9.7 %collective-permute-start = (s32[512]{0:T(512)S(1)}, s32[512]{0:T(512)S(1)}, u32[]{:S(2)}, u32[]{:S(2)}) collective-permute-start(s32[512]{0:T(512)S(1)} %broadcast_add_fusion), channel_id=1, source_target_pairs={{0,4},{1,5},{2,6},{3,7},{4,8},{5,9},{6,10},{7,11},{8,12},{9,13},{1... | collective-permute-start | bytes 6152 | tf_op jit(solution)/shard_map/ppermute | solution.py:23
  40.9 3.9 %collective-permute-start.1 = (s32[512]{0:T(512)S(1)}, s32[512]{0:T(512)S(1)}, u32[]{:S(2)}, u32[]{:S(2)}) collective-permute-start(s32[512]{0:T(512)S(1)} %broadcast_add_fusion), channel_id=1, source_target_pairs={{0,3},{1,4},{2,5},{3,6},{4,7},{5,8},{6,9},{7,10},{8,11},{9,12},{10... | collective-permute-start | bytes 6152 | tf_op jit(solution)/shard_map/ppermute | solution.py:23
  44.8 2.2 collective-permute-start.2
  47.0 2.2 collective-permute-start.3
  49.2 3.3 %stack.2 = bf16[128,512,32]{1,2,0:T(8,128)(2,1)} broadcast(bf16[512,32]{0,1:T(8,128)(2,1)} %param.18), dimensions={1,2} | broadcast | bytes 4227072 | tf_op jit(solution)/shard_map/stack | solution.py:125
  52.5 10.4 %all-to-all-start = ((bf16[128,512,32]{1,2,0:T(8,128)(2,1)}), bf16[128,512,32]{1,2,0:T(8,128)(2,1)}, u32[]{:S(2)}, u32[]{:S(2)}) async-start(bf16[128,512,32]{1,2,0:T(8,128)(2,1)} %stack.2), calls=%async_computation | async-start | bytes 8388608 | tf_op jit(solution)/shard_map/all_to_all | solution.py:124
  63.0 0.7 all-gather.8.cloned.1.call-update
  63.9 3.2 %fusion.17 = f32[512]{0:T(512)S(1)} fusion(bf16[512,4096]{1,0:T(8,128)(2,1)} %param.12), kind=kLoop, calls=%fused_computation.25 | loop fusion | flops 6290944 | bytes 4196352 | tf_op jit(solution)/shard_map/reduce_sum | solution.py:28
  67.2 1.0 multiply_cosine_fusion
  68.2 0.5 slice.36
  68.7 0.6 broadcast_compare_fusion.1
  69.5 0.7 convert_reduce_fusion
  70.2 46.5 %all-gather.4.cloned.1.call-done = bf16[4096,768]{1,0:T(8,128)(2,1)} async-done(((bf16[128,768]{1,0:T(8,128)(2,1)}), bf16[4096,768]{1,0:T(8,128)(2,1)}) %all-gather.4.cloned.1.call-update) | async-done | bytes 6291472 | tf_op jit(solution)/shard_map/all_gather | solution.py:16
  116.7 4.6 %fusion.34 = f32[512,256]{0,1:T(8,128)S(1)} fusion(bf16[4096,768]{1,0:T(8,128)(2,1)} %all-gather.4.cloned.1.call-done, bf16[512,4096]{1,0:T(8,128)(2,1)} %param.12, f32[4096]{0:T(1024)S(1)} %copy-done.8, f32[512]{0:T(512)S(1)} %add_rsqrt_fusion.1), kind=kOutput, calls=%fused_computation.44 | convolution fusion | flops 1082130432 | bytes 6834176 | tf_op jit(solution)/shard_map/dot_general | solution.py:104
  121.3 0.6 fusion.54
  121.9 0.7 pad_maximum_fusion.2
  122.6 1.9 collective-permute-start.4
  124.5 4.3 %collective-permute-start.5 = (bf16[512,256]{0,1:T(8,128)(2,1)}, bf16[512,256]{0,1:T(8,128)(2,1)}, u32[]{:S(2)}, u32[]{:S(2)}) collective-permute-start(bf16[512,256]{0,1:T(8,128)(2,1)} %pad_maximum_fusion.2), channel_id=1, source_target_pairs={{0,3},{1,4},{2,5},{3,6},{4,7},{5,8},{6,9},{7,10},{8,11},{9,12},{10... | collective-permute-start | bytes 786440 | tf_op jit(solution)/shard_map/ppermute | solution.py:23
  128.9 2.2 collective-permute-start.6
  131.1 2.4 collective-permute-start.7
  133.5 2.6 fusion.29
  136.2 0.3 copy.40
  136.5 0.3 copy.41
  137.2 0.3 pad_maximum_fusion.1
  137.5 0.9 fusion.33
  138.4 1.3 fusion.41
  139.8 0.9 fusion.32
  140.7 0.4 collective-permute-done.6
  141.2 4.4 %collective-permute-done.7 = bf16[512,256]{0,1:T(8,128)(2,1)} collective-permute-done((bf16[512,256]{0,1:T(8,128)(2,1)}, bf16[512,256]{0,1:T(8,128)(2,1)}, u32[]{:S(2)}, u32[]{:S(2)}) %collective-permute-start.7) | collective-permute-done | bytes 262176 | tf_op jit(solution)/shard_map/ppermute | solution.py:23
  145.6 1.3 pad_maximum_fusion
  146.9 9.6 %while.14 = (s32[]{:T(128)}, f32[4,512]{1,0:T(4,128)S(1)}, f32[4,512]{1,0:T(4,128)S(1)}, f32[512,4,128]{0,2,1:T(8,128)S(1)}, s32[]{:T(128)}, /*index=5*/s32[2048...) while((s32[]{:T(128)}, f32[4,512]{1,0:T(4,128)S(1)}, ...), condition=%wide.region_8.9_spmd, body=%wide.region_5.8_spmd.sunk | while | flops 549197824 | bytes 33431808 | solution.py:86
  147.9 2.9 %fusion.80 = (f32[4,512]{1,0:T(4,128)S(1)}, f32[512,512,4]{1,0,2:T(8,128)}) fusion(pred[512,512]{0,1:T(8,128)(4,1)S(1)} %broadcast_compare_fusion.3, bf16[512,4,128]{2,0,1:T(8,128)(2,1)S(1)} %get-tuple-element.217, bf16[2048,256]{0,1:T(8,128)(2,1)S(1)} %get-tuple-element.216, s32[]{:T(128)S(6)} %select_n.42), kind=kOutput, calls=%fused_computation.4.clone.1 | convolution fusion | flops 271579136 | bytes 5120004 | tf_op jit(solution)/shard_map/while/body/qhd,kd->hqk/dot_general | solution.py:47
  150.8 3.8 %fusion.83 = f32[512,4,128]{0,2,1:T(8,128)S(1)} fusion(f32[512,512,4]{1,0,2:T(8,128)} %get-tuple-element.177, f32[4,512]{1,0:T(4,128)S(1)} %get-tuple-element.210, pred[512,512]{0,1:T(8,128)(4,1)S(1)} %broadcast_compare_fusion.3, f32[512,4,128]{0,2,1:T(8,128)S(1)} %get-tuple-element.197, f32[512,4]{0,1:T(4,128)S(1)} %get-tuple-element.178, ...), kind=kOutput, calls=%fused_computation.8.clone.1 | convolution fusion | flops 273154048 | bytes 6701064 | tf_op jit(solution)/shard_map/while/body/hqk,kd->qhd/dot_general | solution.py:53
  154.6 0.9 fusion.82
  156.6 5.9 %fusion.20 = bf16[512,4096]{1,0:T(8,128)(2,1)S(1)} fusion(bf16[512,4096]{1,0:T(8,128)(2,1)} %param.12, bf16[512,512]{0,1:T(8,128)(2,1)S(1)} %bitcast.85, bf16[512,4096]{0,1:T(8,128)(2,1)} %bitcast.16), kind=kOutput, calls=%fused_computation.28 | convolution fusion | flops 2153775104 | bytes 13107200 | tf_op jit(solution)/shard_map/dot_general | solution.py:121
  162.5 2.0 copy-done.2
  164.5 0.9 fusion.21
  165.4 27.8 %all-gather.6.cloned.1.call-done = bf16[4096,2048]{1,0:T(8,128)(2,1)} async-done(((bf16[128,2048]{1,0:T(8,128)(2,1)}), bf16[4096,2048]{1,0:T(8,128)(2,1)}) %all-gather.6.cloned.1.call-update) | async-done | bytes 16777232 | tf_op jit(solution)/shard_map/all_gather | solution.py:16
  193.2 8.4 %fusion.27 = f32[512,1024]{1,0:T(8,128)S(1)} fusion(bf16[4096,2048]{1,0:T(8,128)(2,1)} %all-gather.6.cloned.1.call-done, bf16[512,4096]{1,0:T(8,128)(2,1)} %copy-done.2, f32[4096]{0:T(1024)S(1)} %copy-done.9, f32[512]{0:T(512)S(1)} %add_rsqrt_fusion), kind=kOutput, calls=%fused_computation.35 | convolution fusion | flops 4303355904 | bytes 14698496 | tf_op jit(solution)/shard_map/dot_general | solution.py:137
  201.7 2.3 copy-done.6
  203.9 4.7 %multiply_convert_fusion = bf16[512,1024]{1,0:T(8,128)(2,1)S(1)} fusion(f32[512,1024]{1,0:T(8,128)S(1)} %fusion.27, bf16[4096,2048]{1,0:T(8,128)(2,1)S(1)} %copy-done.6, bf16[512,4096]{1,0:T(8,128)(2,1)S(1)} %copy-done.3, f32[4096]{0:T(1024)S(1)} %copy-done.9, f32[512]{0:T(512)S(1)} %add_rsqrt_fusion), kind=kOutput, calls=%fused_computation.46 | convolution fusion | flops 4306501632 | bytes 15747072 | tf_op jit(solution)/shard_map/dot_general | solution.py:138
  208.7 56.8 %all-gather.8.cloned.1.call-done = bf16[1024,4096]{0,1:T(8,128)(2,1)} async-done(((bf16[1024,32]{0,1:T(8,128)(2,1)}), bf16[1024,4096]{0,1:T(8,128)(2,1)}) %all-gather.8.cloned.1.call-update) | async-done | bytes 8388624 | tf_op jit(solution)/shard_map/all_gather | solution.py:142
  265.5 10.2 %fusion.24 = bf16[512,4096]{1,0:T(8,128)(2,1)} fusion(bf16[512,4096]{1,0:T(8,128)(2,1)} %copy-done.2, bf16[512,1024]{1,0:T(8,128)(2,1)S(1)} %multiply_convert_fusion, bf16[1024,4096]{0,1:T(8,128)(2,1)} %all-gather.8.cloned.1.call-done), kind=kOutput, calls=%fused_computation.32 | convolution fusion | flops 4301258752 | bytes 17825792 | tf_op jit(solution)/shard_map/dot_general | solution.py:140
  (53 shorter events, 1.5 us)
Async XLA Ops:
  6.5 110.1 %all-gather.4.cloned.1.call-start = ((), (), s32[]{:S(2)}) async-start(), calls=%async_computation.1 | async-start | bytes 6488064 | tf_op jit(solution)/shard_map/all_gather | solution.py:16
  18.9 174.3 %all-gather.6.cloned.1.call-start = ((), (), s32[]{:S(2)}) async-start(), calls=%async_computation.2 | async-start | bytes 17301504 | tf_op jit(solution)/shard_map/all_gather | solution.py:16
  31.2 37.5 %collective-permute-start = (s32[512]{0:T(512)S(1)}, s32[512]{0:T(512)S(1)}, u32[]{:S(2)}, u32[]{:S(2)}) collective-permute-start(s32[512]{0:T(512)S(1)} %broadcast_add_fusion), channel_id=1, source_target_pairs={{0,4},{1,5},{2,6},{3,7},{4,8},{5,9},{6,10},{7,11},{8,12},{9,13},{1... | collective-permute-start | bytes 6152 | tf_op jit(solution)/shard_map/ppermute | solution.py:23
  40.9 27.8 %collective-permute-start.1 = (s32[512]{0:T(512)S(1)}, s32[512]{0:T(512)S(1)}, u32[]{:S(2)}, u32[]{:S(2)}) collective-permute-start(s32[512]{0:T(512)S(1)} %broadcast_add_fusion), channel_id=1, source_target_pairs={{0,3},{1,4},{2,5},{3,6},{4,7},{5,8},{6,9},{7,10},{8,11},{9,12},{10... | collective-permute-start | bytes 6152 | tf_op jit(solution)/shard_map/ppermute | solution.py:23
  44.8 23.9 %collective-permute-start.2 = (s32[512]{0:T(512)S(1)}, s32[512]{0:T(512)S(1)}, u32[]{:S(2)}, u32[]{:S(2)}) collective-permute-start(s32[512]{0:T(512)S(1)} %broadcast_add_fusion), channel_id=1, source_target_pairs={{0,2},{1,3},{2,4},{3,5},{4,6},{5,7},{6,8},{7,9},{8,10},{9,11},{10,... | collective-permute-start | bytes 6152 | tf_op jit(solution)/shard_map/ppermute | solution.py:23
  47.0 21.7 %collective-permute-start.3 = (s32[512]{0:T(512)S(1)}, s32[512]{0:T(512)S(1)}, u32[]{:S(2)}, u32[]{:S(2)}) collective-permute-start(s32[512]{0:T(512)S(1)} %broadcast_add_fusion), channel_id=1, source_target_pairs={{0,1},{1,2},{2,3},{3,4},{4,5},{5,6},{6,7},{7,8},{8,9},{9,10},{10,1... | collective-permute-start | bytes 6152 | tf_op jit(solution)/shard_map/ppermute | solution.py:23
  52.5 104.1 %all-to-all-start = ((bf16[128,512,32]{1,2,0:T(8,128)(2,1)}), bf16[128,512,32]{1,2,0:T(8,128)(2,1)}, u32[]{:S(2)}, u32[]{:S(2)}) async-start(bf16[128,512,32]{1,2,0:T(8,128)(2,1)} %stack.2), calls=%async_computation | async-start | bytes 8388608 | tf_op jit(solution)/shard_map/all_to_all | solution.py:124
  62.9 53.7 %copy-start.8 = (f32[4096]{0:T(1024)S(1)}, f32[4096]{0:T(1024)}, u32[]{:S(2)}) copy-start(f32[4096]{0:T(1024)} %param.14) | copy-start | bytes 49156
  63.0 202.5 %all-gather.8.cloned.1.call-start = ((), (), s32[]{:S(2)}) async-start(), calls=%async_computation.3 | async-start | bytes 8454144 | tf_op jit(solution)/shard_map/all_gather | solution.py:142
  116.7 16.8 %copy-start.1 = (bf16[512,4096]{1,0:T(8,128)(2,1)S(1)}, bf16[512,4096]{1,0:T(8,128)(2,1)}, u32[]{:S(2)}) copy-start(bf16[512,4096]{1,0:T(8,128)(2,1)} %param.12) | copy-start | bytes 12582916
  116.7 16.8 %copy-start.7 = (bf16[4096,768]{1,0:T(8,128)(2,1)S(1)}, bf16[4096,768]{1,0:T(8,128)(2,1)}, u32[]{:S(2)}) copy-start(bf16[4096,768]{1,0:T(8,128)(2,1)} %all-gather.4.cloned.1.call-done) | copy-start | bytes 18874372
  121.3 9.8 %copy-start.4 = (f32[512,256]{0,1:T(8,128)}, f32[512,256]{0,1:T(8,128)S(1)}, u32[]{:S(2)}) copy-start(f32[512,256]{0,1:T(8,128)S(1)} %fusion.34) | copy-start | bytes 1572868
  122.6 18.1 %collective-permute-start.4 = (bf16[512,256]{0,1:T(8,128)(2,1)}, bf16[512,256]{0,1:T(8,128)(2,1)}, u32[]{:S(2)}, u32[]{:S(2)}) collective-permute-start(bf16[512,256]{0,1:T(8,128)(2,1)} %pad_maximum_fusion.2), channel_id=1, source_target_pairs={{0,4},{1,5},{2,6},{3,7},{4,8},{5,9},{6,10},{7,11},{8,12},{9,13},{1... | collective-permute-start | bytes 786440 | tf_op jit(solution)/shard_map/ppermute | solution.py:23
  124.5 16.2 %collective-permute-start.5 = (bf16[512,256]{0,1:T(8,128)(2,1)}, bf16[512,256]{0,1:T(8,128)(2,1)}, u32[]{:S(2)}, u32[]{:S(2)}) collective-permute-start(bf16[512,256]{0,1:T(8,128)(2,1)} %pad_maximum_fusion.2), channel_id=1, source_target_pairs={{0,3},{1,4},{2,5},{3,6},{4,7},{5,8},{6,9},{7,10},{8,11},{9,12},{10... | collective-permute-start | bytes 786440 | tf_op jit(solution)/shard_map/ppermute | solution.py:23
  128.9 12.3 %collective-permute-start.6 = (bf16[512,256]{0,1:T(8,128)(2,1)}, bf16[512,256]{0,1:T(8,128)(2,1)}, u32[]{:S(2)}, u32[]{:S(2)}) collective-permute-start(bf16[512,256]{0,1:T(8,128)(2,1)} %pad_maximum_fusion.2), channel_id=1, source_target_pairs={{0,2},{1,3},{2,4},{3,5},{4,6},{5,7},{6,8},{7,9},{8,10},{9,11},{10,... | collective-permute-start | bytes 786440 | tf_op jit(solution)/shard_map/ppermute | solution.py:23
  131.1 14.5 %collective-permute-start.7 = (bf16[512,256]{0,1:T(8,128)(2,1)}, bf16[512,256]{0,1:T(8,128)(2,1)}, u32[]{:S(2)}, u32[]{:S(2)}) collective-permute-start(bf16[512,256]{0,1:T(8,128)(2,1)} %pad_maximum_fusion.2), channel_id=1, source_target_pairs={{0,1},{1,2},{2,3},{3,4},{4,5},{5,6},{6,7},{7,8},{8,9},{9,10},{10,1... | collective-permute-start | bytes 786440 | tf_op jit(solution)/shard_map/ppermute | solution.py:23
  137.2 1.3 copy-start.5
  150.8 3.8 %copy-start = (f32[512,512,4]{1,0,2:T(8,128)S(1)}, f32[512,512,4]{1,0,2:T(8,128)}, u32[]{:S(2)}) copy-start(f32[512,512,4]{1,0,2:T(8,128)} %get-tuple-element.177) | copy-start | bytes 12582916 | tf_op jit(solution)/shard_map/while
  162.5 2.0 copy-start.2
  164.5 28.7 %copy-start.9 = (f32[4096]{0:T(1024)S(1)}, f32[4096]{0:T(1024)}, u32[]{:S(2)}) copy-start(f32[4096]{0:T(1024)} %param.15) | copy-start | bytes 49156
  193.2 8.4 %copy-start.3 = (bf16[512,4096]{1,0:T(8,128)(2,1)S(1)}, bf16[512,4096]{1,0:T(8,128)(2,1)}, u32[]{:S(2)}) copy-start(bf16[512,4096]{1,0:T(8,128)(2,1)} %copy-done.2) | copy-start | bytes 12582916
  193.2 10.7 %copy-start.6 = (bf16[4096,2048]{1,0:T(8,128)(2,1)S(1)}, bf16[4096,2048]{1,0:T(8,128)(2,1)}, u32[]{:S(2)}) copy-start(bf16[4096,2048]{1,0:T(8,128)(2,1)} %all-gather.6.cloned.1.call-done) | copy-start | bytes 50331652
Sparse Core Ops, SparseCore 0:
  19.0 97.5 all-gather.3
  118.9 74.2 all-gather.5
  196.4 69.0 all-gather.7
